TPU v7x, 512 devices: a whole 4x8x8 slice. The times are simulated.
512 devices in a mesh: gx: 64 (over y, z), gy: 8 (over x, core).
Axes of the slice: x: 4, y: 8, z: 8, core: 2. Of those that a mesh axis runs over, the one named last changes fastest.
Arguments:
- droplets: float32 [2, 32, 128, 4096], P(None, None, 'gx', 'gy'), as said below
- moves: int32 [2, 32, 128, 4096], P(None, None, 'gx', 'gy'), may hold values from 0 to 8, as said below
- pairing: int32 [2, 32, 128, 4096], P(None, None, 'gx', 'gy'), may hold values from 0 to 31, as said below
- collisions: int32 [2, 16, 128, 4096], P(None, None, 'gx', 'gy'), may hold values from 0 to 3
Outputs:
- droplets_out: float32 [2, 32, 128, 4096], P(None, None, 'gx', 'gy')
- moments: float32 [2, 2, 16], replicated
Inputs may be any that keep to these rules, and one draw needn't show every extreme that they name: `droplets`: entry 0 holds whole-number multiplicities from 24 to below 300, entry 1 masses from 0.05 to 2. `moves`: A code c means a step of c // 3 - 1 along x and c % 3 - 1 along y. In each step, slot and level, all droplets of one y-row take the same x-step and all droplets landing in one x-column take the same y-step, so every cell and slot receives exactly one droplet. `pairing`: for each step and cell, the entries along the slot dimension are a permutation of 0 to 31.
All inputs are finite; a program needn't handle non-finite values.
Results may differ from a plain program's by a relative error of at most 0.0003.
Values sent between devices are 32-bit elements; how exact they have to be, the bound alone decides.
A program may use at most 64 MiB of HBM per device.

v0:
```python
import jax
import jax.numpy as jnp
from jax import lax
from jax.sharding import Mesh
from jax.sharding import PartitionSpec as P

LEVELS = 16
GY = ("gy_0", "gy_1")
GX = ("gx_0", "gx_1")
GX_GY = ("gx_0", "gx_1", "gy_0", "gy_1")
count_unit = 4096.0


def padded(array, sides, width):
    for axis, dim in sides:
        size, length = (lax.axis_size(axis), array.shape[dim])
        up = [(i, (i + 1) % size) for i in range(size)]
        down = [(j, i) for i, j in up]
        last = lax.slice_in_dim(array, length - width, length, axis=dim)
        leading = lax.slice_in_dim(array, 0, width, axis=dim)
        before = lax.ppermute(last, axis, up)
        after = lax.ppermute(leading, axis, down)
        array = jnp.concatenate([before, array, after], axis=dim)
    return array


def over_axes(array, axes):
    for axis in axes:
        array = lax.psum(array, axis)
    return array


def spread(state, codes):
    twos, slots, cols, rows, levels = state.shape
    extended = jnp.zeros((twos, slots, cols + 2, rows + 2, levels), state.dtype)
    for direction in range(9):
        step_x = direction // 3 - 1
        step_y = direction % 3 - 1
        chosen = jnp.where((codes == direction)[None], state, jnp.zeros_like(state))
        extended = extended + jnp.pad(
            chosen, ((0, 0), (0, 0), (1 + step_x, 1 - step_x), (1 + step_y, 1 - step_y), (0, 0))
        )
    return extended


def settle(extended, cols, rows):
    twos, slots, wide, tall, levels = extended.shape
    rims = jnp.stack([extended[:, :, :, 0], extended[:, :, :, rows + 1]], axis=2).reshape(
        twos, slots, 2, (cols + 2) * levels
    )
    got = padded(rims, ((GY, 2),), 1).reshape(twos, slots, 4, cols + 2, levels)
    middle = (
        extended[:, :, :, 1 : rows + 1]
        .at[:, :, :, 0]
        .add(got[:, :, 0])
        .at[:, :, :, rows - 1]
        .add(got[:, :, 3])
    )
    rims = jnp.stack([middle[:, :, 0], middle[:, :, cols + 1]], axis=2).reshape(
        twos, slots, 2, rows * levels
    )
    got = padded(rims, ((GX, 2),), 1).reshape(twos, slots, 4, rows, levels)
    block = (
        middle[:, :, 1 : cols + 1]
        .at[:, :, 0]
        .add(got[:, :, 0])
        .at[:, :, cols - 1]
        .add(got[:, :, 3])
    )
    return block


def collide(first_count, second_count, first_mass, second_mass, tries):
    big_first = first_count >= second_count
    larger = jnp.where(big_first, first_count, second_count)
    smaller = jnp.where(big_first, second_count, first_count)
    larger_mass = jnp.where(big_first, first_mass, second_mass)
    smaller_mass = jnp.where(big_first, second_mass, first_mass)
    taken = jnp.minimum(tries, larger // smaller)
    remain = larger - taken * smaller
    splits = remain == 0
    halved = smaller // 2
    larger_new = jnp.where(splits, halved, remain)
    smaller_new = jnp.where(splits, smaller - halved, smaller)
    grown = smaller_mass + taken.astype(first_mass.dtype) * larger_mass
    larger_mass_new = jnp.where(splits, grown, larger_mass)
    first_new = jnp.where(big_first, larger_new, smaller_new)
    second_new = jnp.where(big_first, smaller_new, larger_new)
    first_mass_new = jnp.where(big_first, larger_mass_new, grown)
    second_mass_new = jnp.where(big_first, grown, larger_mass_new)
    return (first_new, second_new, first_mass_new, second_mass_new)


def pair_column(counts_f, masses, order, tries):
    slots = counts_f.shape[0]
    slot_ids = lax.broadcasted_iota(jnp.int32, (slots, slots, 1), 1)
    hits = order[:, None, :] == slot_ids
    counts = counts_f.astype(jnp.int32)
    counts_p = jnp.sum(jnp.where(hits, counts[None], 0), axis=1)
    masses_p = jnp.sum(jnp.where(hits, masses[None], jnp.zeros_like(masses)[None]), axis=1)
    first_new, second_new, first_mass, second_mass = collide(
        counts_p[0::2], counts_p[1::2], masses_p[0::2], masses_p[1::2], tries
    )
    counts_pair = jnp.stack([first_new, second_new], axis=1).reshape(counts_p.shape)
    masses_pair = jnp.stack([first_mass, second_mass], axis=1).reshape(masses_p.shape)
    counts_new = jnp.sum(jnp.where(hits, counts_pair[:, None], 0), axis=0)
    masses_new = jnp.sum(
        jnp.where(hits, masses_pair[:, None], jnp.zeros_like(masses_pair)[:, None]), axis=0
    )
    return (counts_new.astype(counts_f.dtype), masses_new)


def coalesce(block, order, tries):
    twos, slots, cols, rows, levels = block.shape
    flat = block.reshape(twos, slots, cols, rows * levels)
    results = []
    for column in range(cols):
        counts_new, masses_new = pair_column(
            flat[0, :, column], flat[1, :, column], order[:, column], tries[:, column]
        )
        results.append(jnp.stack([counts_new, masses_new]))
    return jnp.stack(results, axis=2).reshape(block.shape)


def shards(droplets, moves, pairing, collisions):
    twos, slots, cols, flat = droplets.shape
    levels = LEVELS
    rows = flat // levels
    state = droplets.reshape(twos, slots, cols, rows, levels)
    totals = []
    for step in range(moves.shape[0]):
        codes = moves[step].reshape(slots, cols, rows, levels)
        state = settle(spread(state, codes), cols, rows)
        state = coalesce(state, pairing[step], collisions[step])
        count_sum = jnp.sum(state[0], axis=(0, 1, 2))
        liquid_sum = jnp.sum(state[0] * state[1], axis=(0, 1, 2))
        terms = jnp.stack([count_sum, liquid_sum])
        totals.append(over_axes(terms, GX_GY))
    summed = jnp.stack(totals)
    cells_x = cols * lax.axis_size(GX)
    cells_y = rows * lax.axis_size(GY)
    moments = summed / (cells_x * cells_y * count_unit)
    return (state.reshape(droplets.shape), moments)


def solution(mesh):
    torus = Mesh(mesh.devices.reshape(8, 8, 4, 2), ("gx_0", "gx_1", "gy_0", "gy_1"))
    placed = (
        P(None, None, GX, GY),
        P(None, None, GX, GY),
        P(None, None, GX, GY),
        P(None, None, GX, GY),
    )
    return jax.shard_map(
        shards, mesh=torus, in_specs=placed, out_specs=(P(None, None, GX, GY), P()), check_vma=False
    )
```

profile of v0, /device:TPU:1, one launch (start us, length us, event | category | flops | bytes accessed | tf_op | source)
XLA Modules:
  0.0 132.2 jit_solution(4844064748951774139)
XLA Ops:
  0.6 1.0 fusion.55
  1.9 0.8 broadcast_compare_fusion.16
  3.1 1.2 broadcast_select_fusion.17
  5.6 2.6 %collective-permute-start = (f32[2,32,1,64]{1,3,0,2:T(8,128)}, f32[2,32,1,64]{1,3,0,2:T(8,128)}, u32[]{:S(2)}, u32[]{:S(2)}) collective-permute-start(f32[2,32,1,64]{1,3,0,2:T(8,128)} %bitcast.13), channel_id=1, source_target_pairs={{0,1},{1,2},{2,3},{3,4},{4,5},{5,6},{6,7},{7,0},{8,9},{9,10},{10,1... | collective-permute-start | bytes 49160 | tf_op jit(solution)/shard_map/ppermute | solution.py:21
  8.1 4.3 %collective-permute-start.1 = (f32[2,32,1,64]{1,3,0,2:T(8,128)}, f32[2,32,1,64]{1,3,0,2:T(8,128)}, u32[]{:S(2)}, u32[]{:S(2)}) collective-permute-start(f32[2,32,1,64]{1,3,0,2:T(8,128)} %bitcast.16), channel_id=1, source_target_pairs={{1,0},{2,1},{3,2},{4,3},{5,4},{6,5},{7,6},{0,7},{9,8},{10,9},{11,1... | collective-permute-start | bytes 49160 | tf_op jit(solution)/shard_map/ppermute | solution.py:22
  12.4 0.7 slice_bitcast_fusion.5
  13.3 1.5 %broadcast_compare_fusion.17 = (pred[1,32,2,512]{1,3,2,0:T(8,128)(4,1)}, pred[1,32,2,512]{1,3,2,0:T(8,128)(4,1)S(1)}, pred[1,32,2,512]{1,3,2,0:T(8,128)(4,1)S(1)...) fusion(s32[1,32,2,512]{1,3,2,0:T(8,128)S(1)} %copy.114), kind=kLoop, calls=%fused_computation.87 | loop fusion | flops 294912 | bytes 425984 | tf_op jit(solution)/shard_map/eq | solution.py:39
  14.8 1.3 %fusion.56 = (s32[32,1,512]{2,1,0:T(1,128)S(1)}, s32[32,1,512]{2,1,0:T(1,128)S(1)}, s32[32,1,512]{2,1,0:T(1,128)S(1)}, s32[32,1,512]{2,1,0:T(1,128)S(1)}) fusion(s32[32,2,512]{2,1,0:T(2,128)} %get-tuple-element.172, s32[32,2,512]{2,1,0:T(2,128)} %get-tuple-element.173), kind=kLoop, calls=%fused_computation.232 | loop fusion | bytes 524288 | tf_op jit(solution)/shard_map/slice | solution.py:119
  16.1 0.9 fusion.57
  17.2 0.8 fusion.18
  18.1 0.9 fusion.17
  19.2 1.9 %collective-permute-start.2 = (f32[2,32,1,512]{1,3,2,0:T(8,128)S(1)}, f32[2,32,1,512]{1,3,2,0:T(8,128)S(1)}, u32[]{:S(2)}, u32[]{:S(2)}) collective-permute-start(f32[2,32,1,512]{1,3,2,0:T(8,128)S(1)} %get-tuple-element.144), channel_id=1, source_target_pairs={{0,8},{8,16},{16,24},{24,32},{32,40},{40,48},{48,56},{56,64},{64,7... | collective-permute-start | bytes 393224 | tf_op jit(solution)/shard_map/ppermute | solution.py:21
  21.3 9.5 %collective-permute-start.3 = (f32[2,32,1,512]{1,3,2,0:T(8,128)S(1)}, f32[2,32,1,512]{1,3,2,0:T(8,128)S(1)}, u32[]{:S(2)}, u32[]{:S(2)}) collective-permute-start(f32[2,32,1,512]{1,3,2,0:T(8,128)S(1)} %get-tuple-element.143), channel_id=1, source_target_pairs={{8,0},{16,8},{24,16},{32,24},{40,32},{48,40},{56,48},{64,56},{72,6... | collective-permute-start | bytes 393224 | tf_op jit(solution)/shard_map/ppermute | solution.py:22
  30.8 8.2 %collective-permute-done.2 = f32[2,32,1,512]{1,3,2,0:T(8,128)S(1)} collective-permute-done((f32[2,32,1,512]{1,3,2,0:T(8,128)S(1)}, f32[2,32,1,512]{1,3,2,0:T(8,128)S(1)}, u32[]{:S(2)}, u32[]{:S(2)}) %collective-permute-start.2) | collective-permute-done | bytes 131104 | tf_op jit(solution)/shard_map/ppermute | solution.py:21
  39.0 0.9 collective-permute-done.3
  42.5 0.8 select_bitcast_fusion.7
  43.8 0.7 fusion.19
  48.9 3.8 %collective-permute-start.4 = (f32[2,32,1,64]{1,3,0,2:T(8,128)S(1)}, f32[2,32,1,64]{1,3,0,2:T(8,128)S(1)}, u32[]{:S(2)}, u32[]{:S(2)}) collective-permute-start(f32[2,32,1,64]{1,3,0,2:T(8,128)S(1)} %bitcast.263), channel_id=1, source_target_pairs={{0,1},{1,2},{2,3},{3,4},{4,5},{5,6},{6,7},{7,0},{8,9},{9,10},{10,1... | collective-permute-start | bytes 49160 | tf_op jit(solution)/shard_map/ppermute | solution.py:21
  52.9 1.2 collective-permute-done.4
  54.1 2.3 %collective-permute-done.5 = f32[2,32,1,64]{1,3,0,2:T(8,128)S(1)} collective-permute-done((f32[2,32,1,64]{1,3,0,2:T(8,128)S(1)}, f32[2,32,1,64]{1,3,0,2:T(8,128)S(1)}, u32[]{:S(2)}, u32[]{:S(2)}) %collective-permute-start.5) | collective-permute-done | bytes 16416 | tf_op jit(solution)/shard_map/ppermute | solution.py:22
  56.6 0.9 fusion.53
  57.5 1.9 %collective-permute-start.6 = (f32[2,32,1,512]{1,3,2,0:T(8,128)}, f32[2,32,1,512]{1,3,2,0:T(8,128)S(1)}, u32[]{:S(2)}, u32[]{:S(2)}) collective-permute-start(f32[2,32,1,512]{1,3,2,0:T(8,128)} %get-tuple-element.129), channel_id=1, source_target_pairs={{0,8},{8,16},{16,24},{24,32},{32,40},{40,48},{48,56},{56,64},{64,7... | collective-permute-start | bytes 393224 | tf_op jit(solution)/shard_map/ppermute | solution.py:21
  59.8 7.7 %collective-permute-start.7 = (f32[2,32,1,512]{1,3,2,0:T(8,128)S(1)}, f32[2,32,1,512]{1,3,2,0:T(8,128)S(1)}, u32[]{:S(2)}, u32[]{:S(2)}) collective-permute-start(f32[2,32,1,512]{1,3,2,0:T(8,128)S(1)} %get-tuple-element.128), channel_id=1, source_target_pairs={{8,0},{16,8},{24,16},{32,24},{40,32},{48,40},{56,48},{64,56},{72,6... | collective-permute-start | bytes 393224 | tf_op jit(solution)/shard_map/ppermute | solution.py:22
  67.4 9.8 %collective-permute-done.6 = f32[2,32,1,512]{1,3,2,0:T(8,128)S(1)} collective-permute-done((f32[2,32,1,512]{1,3,2,0:T(8,128)}, f32[2,32,1,512]{1,3,2,0:T(8,128)S(1)}, u32[]{:S(2)}, u32[]{:S(2)}) %collective-permute-start.6) | collective-permute-done | bytes 131104 | tf_op jit(solution)/shard_map/ppermute | solution.py:21
  77.3 1.0 collective-permute-done.7
  80.8 0.8 select_bitcast_fusion.3
  82.1 0.7 fusion.23
  84.6 0.9 copy.109
  85.6 10.7 %all-reduce.19 = (f32[2,16]{1,0:T(2,128)S(1)}, f32[2,16]{1,0:T(2,128)S(1)}) all-reduce(f32[2,16]{1,0:T(2,128)S(1)} %pad_maximum_fusion.9, f32[2,16]{1,0:T(2,128)S(1)} %pad_maximum_fusion.8), channel_id=1, replica_groups=mesh['gx_0'=8,'gx_1'=8,'gy_0'=4,'gy_1'=2] {'gx_0'}, use_global_device_ids=true, to_apply=%region_28.29 | all-reduce | flops 64 | bytes 512 | tf_op jit(solution)/shard_map/psum | solution.py:29
  96.2 16.4 %all-reduce.18 = (f32[2,16]{1,0:T(2,128)S(1)}, f32[2,16]{1,0:T(2,128)S(1)}) all-reduce(f32[2,16]{1,0:T(2,128)S(1)} %get-tuple-element.110, f32[2,16]{1,0:T(2,128)S(1)} %get-tuple-element.111), channel_id=1, replica_groups=mesh['gx_0'=8,'gx_1'=8,'gy_0'=4,'gy_1'=2] {'gx_1'}, use_global_device_ids=true, to_apply=%region_29.30 | all-reduce | flops 64 | bytes 512 | tf_op jit(solution)/shard_map/psum | solution.py:29
  112.7 7.5 %all-reduce.20 = (f32[2,16]{1,0:T(2,128)S(1)}, f32[2,16]{1,0:T(2,128)S(1)}) all-reduce(f32[2,16]{1,0:T(2,128)S(1)} %get-tuple-element.108, f32[2,16]{1,0:T(2,128)S(1)} %get-tuple-element.109), channel_id=1, replica_groups=mesh['gx_0'=8,'gx_1'=8,'gy_0'=4,'gy_1'=2] {'gy_0'}, use_global_device_ids=true, to_apply=%region_30.31 | all-reduce | flops 64 | bytes 512 | tf_op jit(solution)/shard_map/psum | solution.py:29
  120.1 11.4 %all-reduce.21 = (f32[1,2,16]{2,1,0:T(2,128)S(1)}, f32[1,2,16]{2,1,0:T(2,128)S(1)}) all-reduce(f32[1,2,16]{2,1,0:T(2,128)S(1)} %bitcast.268, f32[1,2,16]{2,1,0:T(2,128)S(1)} %bitcast.269), channel_id=1, replica_groups=mesh['gx_0'=8,'gx_1'=8,'gy_0'=4,'gy_1'=2] {'gy_1'}, use_global_device_ids=true, to_apply=%region_31.32 | all-reduce | flops 64 | bytes 512 | tf_op jit(solution)/shard_map/psum | solution.py:29
  (137 shorter events, 15.7 us)
Async XLA Ops:
  0.6 2.1 %copy-start.3 = (f32[2,32,2,512]{3,2,1,0:T(2,128)S(1)}, f32[2,32,2,512]{3,2,1,0:T(2,128)}, u32[]{:S(2)}) copy-start(f32[2,32,2,512]{3,2,1,0:T(2,128)} %param.20) | copy-start | bytes 786436
  4.3 8.1 %copy-start.4 = (s32[2,32,2,512]{3,2,1,0:T(2,128)S(1)}, s32[2,32,2,512]{3,2,1,0:T(2,128)}, u32[]{:S(2)}) copy-start(s32[2,32,2,512]{3,2,1,0:T(2,128)} %param.22) | copy-start | bytes 786436
  5.6 11.7 %collective-permute-start = (f32[2,32,1,64]{1,3,0,2:T(8,128)}, f32[2,32,1,64]{1,3,0,2:T(8,128)}, u32[]{:S(2)}, u32[]{:S(2)}) collective-permute-start(f32[2,32,1,64]{1,3,0,2:T(8,128)} %bitcast.13), channel_id=1, source_target_pairs={{0,1},{1,2},{2,3},{3,4},{4,5},{5,6},{6,7},{7,0},{8,9},{9,10},{10,1... | collective-permute-start | bytes 49160 | tf_op jit(solution)/shard_map/ppermute | solution.py:21
  8.1 9.9 %collective-permute-start.1 = (f32[2,32,1,64]{1,3,0,2:T(8,128)}, f32[2,32,1,64]{1,3,0,2:T(8,128)}, u32[]{:S(2)}, u32[]{:S(2)}) collective-permute-start(f32[2,32,1,64]{1,3,0,2:T(8,128)} %bitcast.16), channel_id=1, source_target_pairs={{1,0},{2,1},{3,2},{4,3},{5,4},{6,5},{7,6},{0,7},{9,8},{10,9},{11,1... | collective-permute-start | bytes 49160 | tf_op jit(solution)/shard_map/ppermute | solution.py:22
  19.2 19.8 %collective-permute-start.2 = (f32[2,32,1,512]{1,3,2,0:T(8,128)S(1)}, f32[2,32,1,512]{1,3,2,0:T(8,128)S(1)}, u32[]{:S(2)}, u32[]{:S(2)}) collective-permute-start(f32[2,32,1,512]{1,3,2,0:T(8,128)S(1)} %get-tuple-element.144), channel_id=1, source_target_pairs={{0,8},{8,16},{16,24},{24,32},{32,40},{40,48},{48,56},{56,64},{64,7... | collective-permute-start | bytes 393224 | tf_op jit(solution)/shard_map/ppermute | solution.py:21
  21.3 18.7 %collective-permute-start.3 = (f32[2,32,1,512]{1,3,2,0:T(8,128)S(1)}, f32[2,32,1,512]{1,3,2,0:T(8,128)S(1)}, u32[]{:S(2)}, u32[]{:S(2)}) collective-permute-start(f32[2,32,1,512]{1,3,2,0:T(8,128)S(1)} %get-tuple-element.143), channel_id=1, source_target_pairs={{8,0},{16,8},{24,16},{32,24},{40,32},{48,40},{56,48},{64,56},{72,6... | collective-permute-start | bytes 393224 | tf_op jit(solution)/shard_map/ppermute | solution.py:22
  43.4 3.8 %copy-start = (pred[1,32,2,512]{1,3,2,0:T(8,128)(4,1)S(1)}, pred[1,32,2,512]{1,3,2,0:T(8,128)(4,1)}, u32[]{:S(2)}) copy-start(pred[1,32,2,512]{1,3,2,0:T(8,128)(4,1)} %get-tuple-element.154) | copy-start | bytes 98308
  43.4 3.8 %copy-start.1 = (pred[1,32,2,512]{1,3,2,0:T(8,128)(4,1)S(1)}, pred[1,32,2,512]{1,3,2,0:T(8,128)(4,1)}, u32[]{:S(2)}) copy-start(pred[1,32,2,512]{1,3,2,0:T(8,128)(4,1)} %get-tuple-element.161) | copy-start | bytes 98308
  43.4 3.8 %copy-start.2 = (pred[1,32,2,512]{1,3,2,0:T(8,128)(4,1)S(1)}, pred[1,32,2,512]{1,3,2,0:T(8,128)(4,1)}, u32[]{:S(2)}) copy-start(pred[1,32,2,512]{1,3,2,0:T(8,128)(4,1)} %get-tuple-element.162) | copy-start | bytes 98308
  48.9 5.2 %collective-permute-start.4 = (f32[2,32,1,64]{1,3,0,2:T(8,128)S(1)}, f32[2,32,1,64]{1,3,0,2:T(8,128)S(1)}, u32[]{:S(2)}, u32[]{:S(2)}) collective-permute-start(f32[2,32,1,64]{1,3,0,2:T(8,128)S(1)} %bitcast.263), channel_id=1, source_target_pairs={{0,1},{1,2},{2,3},{3,4},{4,5},{5,6},{6,7},{7,0},{8,9},{9,10},{10,1... | collective-permute-start | bytes 49160 | tf_op jit(solution)/shard_map/ppermute | solution.py:21
  52.7 3.7 %collective-permute-start.5 = (f32[2,32,1,64]{1,3,0,2:T(8,128)S(1)}, f32[2,32,1,64]{1,3,0,2:T(8,128)S(1)}, u32[]{:S(2)}, u32[]{:S(2)}) collective-permute-start(f32[2,32,1,64]{1,3,0,2:T(8,128)S(1)} %bitcast.262), channel_id=1, source_target_pairs={{1,0},{2,1},{3,2},{4,3},{5,4},{6,5},{7,6},{0,7},{9,8},{10,9},{11,1... | collective-permute-start | bytes 49160 | tf_op jit(solution)/shard_map/ppermute | solution.py:22
  56.5 2.9 %copy-start.5 = (f32[1,32,512]{2,1,0:T(8,128)S(1)}, f32[1,32,512]{2,1,0:T(8,128)}, u32[]{:S(2)}) copy-start(f32[1,32,512]{2,1,0:T(8,128)} %get-tuple-element.200) | copy-start | bytes 196612
  57.5 19.8 %collective-permute-start.6 = (f32[2,32,1,512]{1,3,2,0:T(8,128)}, f32[2,32,1,512]{1,3,2,0:T(8,128)S(1)}, u32[]{:S(2)}, u32[]{:S(2)}) collective-permute-start(f32[2,32,1,512]{1,3,2,0:T(8,128)} %get-tuple-element.129), channel_id=1, source_target_pairs={{0,8},{8,16},{16,24},{24,32},{32,40},{40,48},{48,56},{56,64},{64,7... | collective-permute-start | bytes 393224 | tf_op jit(solution)/shard_map/ppermute | solution.py:21
  59.8 18.6 %collective-permute-start.7 = (f32[2,32,1,512]{1,3,2,0:T(8,128)S(1)}, f32[2,32,1,512]{1,3,2,0:T(8,128)S(1)}, u32[]{:S(2)}, u32[]{:S(2)}) collective-permute-start(f32[2,32,1,512]{1,3,2,0:T(8,128)S(1)} %get-tuple-element.128), channel_id=1, source_target_pairs={{8,0},{16,8},{24,16},{32,24},{40,32},{48,40},{56,48},{64,56},{72,6... | collective-permute-start | bytes 393224 | tf_op jit(solution)/shard_map/ppermute | solution.py:22
where the time goes:
time: 133 us; the launch traced here: 132 us
  blocking collectives  46 us (35%)
  starting transfers between devices  31.6 us (24%)
  waiting for transfers between devices  23.5 us (18%)
  other arithmetic  19 us (14%)
  local copies, waits for them, and re-layouts  10.6 us (8%)
  between operations  1.4 us (1%)
    psum x4, blocking collectives, over_axes(): array = lax.psum(array, axis)  46 us
    ppermute x4, starting transfers between devices, padded(): after = lax.ppermute(leading, axis, down)  21.4 us
    ppermute x4, waiting for transfers between devices, padded(): before = lax.ppermute(last, axis, up)  19.2 us
    ppermute x4, starting transfers between devices, padded(): before = lax.ppermute(last, axis, up)  10.2 us
    ppermute x4, waiting for transfers between devices, padded(): after = lax.ppermute(leading, axis, down)  4.28 us
  transfers between devices with their start and end apart: 8, of which 6 were waited for; matrix products, arithmetic and copies ran while one was open for 5% of the time, Pallas kernels for 0%

commit v1 on v0

--- a/solution.py
+++ b/solution.py
@@ -26,7 +26,7 @@
 
 def over_axes(array, axes):
     for axis in axes:
-        array = lax.psum(array, axis)
+        array = jnp.sum(lax.all_gather(array, axis), axis=0)
     return array
 
 

time: 133 us -> 175 us (1.32)
  blocking collectives: 46 us -> 91.9 us
  starting transfers between devices: 31.6 us -> 26.9 us
    all_gather x0 -> x8, blocking collectives: none -> 91.9 us  [over_axes(): array = jnp.sum(lax.all_gather(array, axis), axis=0)]
    psum x4 -> x0, blocking collectives: 46 us -> none  [over_axes(): array = lax.psum(array, axis)]
    ppermute x4, waiting for transfers between devices: 4.28 us -> 15.3 us  [padded(): after = lax.ppermute(leading, axis, down)]
    ppermute x4, waiting for transfers between devices: 19.2 us -> 9.38 us  [padded(): before = lax.ppermute(last, axis, up)]
    ppermute x4, starting transfers between devices: 21.4 us -> 16.7 us  [padded(): after = lax.ppermute(leading, axis, down)]
  transfers between devices with their start and end apart: 8 -> 8, of which waited for: 6 -> 5; matrix products, arithmetic and copies ran while one was open for 5% -> 4% of each run, Pallas kernels for 0% -> 0%
where the time goes in v1:
time: 175 us
  blocking collectives  91.9 us (53%)
  starting transfers between devices  26.9 us (15%)
  waiting for transfers between devices  24.7 us (14%)
  other arithmetic  19.1 us (11%)
  local copies, waits for them, and re-layouts  10.6 us (6%)
    all_gather x8, blocking collectives, over_axes(): array = jnp.sum(lax.all_gather(array, axis), axis=0)  91.9 us
    ppermute x4, starting transfers between devices, padded(): after = lax.ppermute(leading, axis, down)  16.7 us
    ppermute x4, waiting for transfers between devices, padded(): after = lax.ppermute(leading, axis, down)  15.3 us
    ppermute x4, starting transfers between devices, padded(): before = lax.ppermute(last, axis, up)  10.2 us
    ppermute x4, waiting for transfers between devices, padded(): before = lax.ppermute(last, axis, up)  9.38 us
  transfers between devices with their start and end apart: 8, of which 5 were waited for; matrix products, arithmetic and copies ran while one was open for 4% of the time, Pallas kernels for 0%

profile of v1, /device:TPU:1, one launch (start us, length us, event | category | flops | bytes accessed | tf_op | source)
XLA Modules:
  0.0 174.6 jit_solution(8606014410866812216)
XLA Ops:
  0.6 1.0 fusion.55
  1.9 0.8 broadcast_compare_fusion.16
  3.1 1.2 broadcast_select_fusion.17
  5.6 2.6 %collective-permute-start = (f32[2,32,1,64]{1,3,0,2:T(8,128)}, f32[2,32,1,64]{1,3,0,2:T(8,128)}, u32[]{:S(2)}, u32[]{:S(2)}) collective-permute-start(f32[2,32,1,64]{1,3,0,2:T(8,128)} %bitcast.13), channel_id=1, source_target_pairs={{0,1},{1,2},{2,3},{3,4},{4,5},{5,6},{6,7},{7,0},{8,9},{9,10},{10,1... | collective-permute-start | bytes 49160 | tf_op jit(solution)/shard_map/ppermute | solution.py:21
  8.1 4.3 %collective-permute-start.1 = (f32[2,32,1,64]{1,3,0,2:T(8,128)}, f32[2,32,1,64]{1,3,0,2:T(8,128)}, u32[]{:S(2)}, u32[]{:S(2)}) collective-permute-start(f32[2,32,1,64]{1,3,0,2:T(8,128)} %bitcast.16), channel_id=1, source_target_pairs={{1,0},{2,1},{3,2},{4,3},{5,4},{6,5},{7,6},{0,7},{9,8},{10,9},{11,1... | collective-permute-start | bytes 49160 | tf_op jit(solution)/shard_map/ppermute | solution.py:22
  13.3 1.5 broadcast_compare_fusion.17
  14.8 1.3 fusion.56
  16.1 0.9 fusion.57
  17.2 0.8 fusion.18
  18.1 0.9 fusion.17
  19.2 1.9 %collective-permute-start.2 = (f32[2,32,1,512]{1,3,2,0:T(8,128)S(1)}, f32[2,32,1,512]{1,3,2,0:T(8,128)S(1)}, u32[]{:S(2)}, u32[]{:S(2)}) collective-permute-start(f32[2,32,1,512]{1,3,2,0:T(8,128)S(1)} %get-tuple-element.136), channel_id=1, source_target_pairs={{0,8},{8,16},{16,24},{24,32},{32,40},{40,48},{48,56},{56,64},{64,7... | collective-permute-start | bytes 393224 | tf_op jit(solution)/shard_map/ppermute | solution.py:21
  21.3 9.5 %collective-permute-start.3 = (f32[2,32,1,512]{1,3,2,0:T(8,128)S(1)}, f32[2,32,1,512]{1,3,2,0:T(8,128)S(1)}, u32[]{:S(2)}, u32[]{:S(2)}) collective-permute-start(f32[2,32,1,512]{1,3,2,0:T(8,128)S(1)} %get-tuple-element.135), channel_id=1, source_target_pairs={{8,0},{16,8},{24,16},{32,24},{40,32},{48,40},{56,48},{64,56},{72,6... | collective-permute-start | bytes 393224 | tf_op jit(solution)/shard_map/ppermute | solution.py:22
  30.8 8.2 %collective-permute-done.2 = f32[2,32,1,512]{1,3,2,0:T(8,128)S(1)} collective-permute-done((f32[2,32,1,512]{1,3,2,0:T(8,128)S(1)}, f32[2,32,1,512]{1,3,2,0:T(8,128)S(1)}, u32[]{:S(2)}, u32[]{:S(2)}) %collective-permute-start.2) | collective-permute-done | bytes 131104 | tf_op jit(solution)/shard_map/ppermute | solution.py:21
  39.0 0.9 collective-permute-done.3
  42.5 0.8 select_bitcast_fusion.7
  48.9 3.8 %collective-permute-start.4 = (f32[2,32,1,64]{1,3,0,2:T(8,128)S(1)}, f32[2,32,1,64]{1,3,0,2:T(8,128)S(1)}, u32[]{:S(2)}, u32[]{:S(2)}) collective-permute-start(f32[2,32,1,64]{1,3,0,2:T(8,128)S(1)} %bitcast.273), channel_id=1, source_target_pairs={{0,1},{1,2},{2,3},{3,4},{4,5},{5,6},{6,7},{7,0},{8,9},{9,10},{10,1... | collective-permute-start | bytes 49160 | tf_op jit(solution)/shard_map/ppermute | solution.py:21
  52.9 1.2 collective-permute-done.4
  54.1 2.3 %collective-permute-done.5 = f32[2,32,1,64]{1,3,0,2:T(8,128)S(1)} collective-permute-done((f32[2,32,1,64]{1,3,0,2:T(8,128)S(1)}, f32[2,32,1,64]{1,3,0,2:T(8,128)S(1)}, u32[]{:S(2)}, u32[]{:S(2)}) %collective-permute-start.5) | collective-permute-done | bytes 16416 | tf_op jit(solution)/shard_map/ppermute | solution.py:22
  56.6 0.9 fusion.53
  57.5 1.9 %collective-permute-start.6 = (f32[2,32,1,512]{1,3,2,0:T(8,128)}, f32[2,32,1,512]{1,3,2,0:T(8,128)S(1)}, u32[]{:S(2)}, u32[]{:S(2)}) collective-permute-start(f32[2,32,1,512]{1,3,2,0:T(8,128)} %get-tuple-element.121), channel_id=1, source_target_pairs={{0,8},{8,16},{16,24},{24,32},{32,40},{40,48},{48,56},{56,64},{64,7... | collective-permute-start | bytes 393224 | tf_op jit(solution)/shard_map/ppermute | solution.py:21
  59.7 11.5 %all-gather.8 = f32[8,2,16]{2,1,0:T(2,128)S(1)} all-gather(f32[1,2,16]{2,1,0:T(2,128)S(1)} %maximum_bitcast_fusion.4), channel_id=2, replica_groups=mesh['gx_0'=8,'gx_1'=8,'gy_0'=4,'gy_1'=2] {'gx_0'}, dimensions={0}, use_global_device_ids=true | all-gather | bytes 1152 | tf_op jit(solution)/shard_map/all_gather | solution.py:29
  71.2 22.0 %all-gather.9 = f32[8,2,16]{2,1,0:T(2,128)S(1)} all-gather(f32[1,2,16]{2,1,0:T(2,128)S(1)} %bitcast.274), channel_id=3, replica_groups=mesh['gx_0'=8,'gx_1'=8,'gy_0'=4,'gy_1'=2] {'gx_1'}, dimensions={0}, use_global_device_ids=true | all-gather | bytes 1152 | tf_op jit(solution)/shard_map/all_gather | solution.py:29
  93.2 5.8 %all-gather.10 = f32[4,2,16]{2,1,0:T(2,128)S(1)} all-gather(f32[1,2,16]{2,1,0:T(2,128)S(1)} %bitcast.275), channel_id=4, replica_groups=mesh['gx_0'=8,'gx_1'=8,'gy_0'=4,'gy_1'=2] {'gy_0'}, dimensions={0}, use_global_device_ids=true | all-gather | bytes 640 | tf_op jit(solution)/shard_map/all_gather | solution.py:29
  99.1 9.3 %all-gather.11 = f32[2,2,16]{2,1,0:T(2,128)S(1)} all-gather(f32[1,2,16]{2,1,0:T(2,128)S(1)} %bitcast.280), channel_id=5, replica_groups=mesh['gx_0'=8,'gx_1'=8,'gy_0'=4,'gy_1'=2] {'gy_1'}, dimensions={0}, use_global_device_ids=true | all-gather | bytes 384 | tf_op jit(solution)/shard_map/all_gather | solution.py:29
  108.5 2.9 %collective-permute-start.7 = (f32[2,32,1,512]{1,3,2,0:T(8,128)S(1)}, f32[2,32,1,512]{1,3,2,0:T(8,128)S(1)}, u32[]{:S(2)}, u32[]{:S(2)}) collective-permute-start(f32[2,32,1,512]{1,3,2,0:T(8,128)S(1)} %get-tuple-element.120), channel_id=1, source_target_pairs={{8,0},{16,8},{24,16},{32,24},{40,32},{48,40},{56,48},{64,56},{72,6... | collective-permute-start | bytes 393224 | tf_op jit(solution)/shard_map/ppermute | solution.py:22
  111.5 12.0 %collective-permute-done.7 = f32[2,32,1,512]{1,3,2,0:T(8,128)S(1)} collective-permute-done((f32[2,32,1,512]{1,3,2,0:T(8,128)S(1)}, f32[2,32,1,512]{1,3,2,0:T(8,128)S(1)}, u32[]{:S(2)}, u32[]{:S(2)}) %collective-permute-start.7) | collective-permute-done | bytes 131104 | tf_op jit(solution)/shard_map/ppermute | solution.py:22
  126.0 0.8 select_bitcast_fusion.3
  129.9 11.7 %all-gather.12 = f32[8,2,16]{2,1,0:T(2,128)S(1)} all-gather(f32[1,2,16]{2,1,0:T(2,128)S(1)} %maximum_bitcast_fusion.5), channel_id=6, replica_groups=mesh['gx_0'=8,'gx_1'=8,'gy_0'=4,'gy_1'=2] {'gx_0'}, dimensions={0}, use_global_device_ids=true | all-gather | bytes 1152 | tf_op jit(solution)/shard_map/all_gather | solution.py:29
  141.6 12.6 %all-gather.13 = f32[8,2,16]{2,1,0:T(2,128)S(1)} all-gather(f32[1,2,16]{2,1,0:T(2,128)S(1)} %bitcast.276), channel_id=7, replica_groups=mesh['gx_0'=8,'gx_1'=8,'gy_0'=4,'gy_1'=2] {'gx_1'}, dimensions={0}, use_global_device_ids=true | all-gather | bytes 1152 | tf_op jit(solution)/shard_map/all_gather | solution.py:29
  154.2 7.0 %all-gather.14 = f32[4,2,16]{2,1,0:T(2,128)S(1)} all-gather(f32[1,2,16]{2,1,0:T(2,128)S(1)} %bitcast.277), channel_id=8, replica_groups=mesh['gx_0'=8,'gx_1'=8,'gy_0'=4,'gy_1'=2] {'gy_0'}, dimensions={0}, use_global_device_ids=true | all-gather | bytes 640 | tf_op jit(solution)/shard_map/all_gather | solution.py:29
  161.2 11.9 %all-gather.15 = f32[2,2,16]{2,1,0:T(2,128)S(1)} all-gather(f32[1,2,16]{2,1,0:T(2,128)S(1)} %bitcast.281), channel_id=9, replica_groups=mesh['gx_0'=8,'gx_1'=8,'gy_0'=4,'gy_1'=2] {'gy_1'}, dimensions={0}, use_global_device_ids=true | all-gather | bytes 384 | tf_op jit(solution)/shard_map/all_gather | solution.py:29
  173.1 0.9 copy.109
  (149 shorter events, 18.1 us)
Async XLA Ops:
  0.6 2.1 %copy-start.3 = (f32[2,32,2,512]{3,2,1,0:T(2,128)S(1)}, f32[2,32,2,512]{3,2,1,0:T(2,128)}, u32[]{:S(2)}) copy-start(f32[2,32,2,512]{3,2,1,0:T(2,128)} %param.20) | copy-start | bytes 786436
  4.3 8.1 %copy-start.4 = (s32[2,32,2,512]{3,2,1,0:T(2,128)S(1)}, s32[2,32,2,512]{3,2,1,0:T(2,128)}, u32[]{:S(2)}) copy-start(s32[2,32,2,512]{3,2,1,0:T(2,128)} %param.22) | copy-start | bytes 786436
  5.6 11.7 %collective-permute-start = (f32[2,32,1,64]{1,3,0,2:T(8,128)}, f32[2,32,1,64]{1,3,0,2:T(8,128)}, u32[]{:S(2)}, u32[]{:S(2)}) collective-permute-start(f32[2,32,1,64]{1,3,0,2:T(8,128)} %bitcast.13), channel_id=1, source_target_pairs={{0,1},{1,2},{2,3},{3,4},{4,5},{5,6},{6,7},{7,0},{8,9},{9,10},{10,1... | collective-permute-start | bytes 49160 | tf_op jit(solution)/shard_map/ppermute | solution.py:21
  8.1 9.9 %collective-permute-start.1 = (f32[2,32,1,64]{1,3,0,2:T(8,128)}, f32[2,32,1,64]{1,3,0,2:T(8,128)}, u32[]{:S(2)}, u32[]{:S(2)}) collective-permute-start(f32[2,32,1,64]{1,3,0,2:T(8,128)} %bitcast.16), channel_id=1, source_target_pairs={{1,0},{2,1},{3,2},{4,3},{5,4},{6,5},{7,6},{0,7},{9,8},{10,9},{11,1... | collective-permute-start | bytes 49160 | tf_op jit(solution)/shard_map/ppermute | solution.py:22
  19.2 19.8 %collective-permute-start.2 = (f32[2,32,1,512]{1,3,2,0:T(8,128)S(1)}, f32[2,32,1,512]{1,3,2,0:T(8,128)S(1)}, u32[]{:S(2)}, u32[]{:S(2)}) collective-permute-start(f32[2,32,1,512]{1,3,2,0:T(8,128)S(1)} %get-tuple-element.136), channel_id=1, source_target_pairs={{0,8},{8,16},{16,24},{24,32},{32,40},{40,48},{48,56},{56,64},{64,7... | collective-permute-start | bytes 393224 | tf_op jit(solution)/shard_map/ppermute | solution.py:21
  21.3 18.7 %collective-permute-start.3 = (f32[2,32,1,512]{1,3,2,0:T(8,128)S(1)}, f32[2,32,1,512]{1,3,2,0:T(8,128)S(1)}, u32[]{:S(2)}, u32[]{:S(2)}) collective-permute-start(f32[2,32,1,512]{1,3,2,0:T(8,128)S(1)} %get-tuple-element.135), channel_id=1, source_target_pairs={{8,0},{16,8},{24,16},{32,24},{40,32},{48,40},{56,48},{64,56},{72,6... | collective-permute-start | bytes 393224 | tf_op jit(solution)/shard_map/ppermute | solution.py:22
  43.4 3.8 %copy-start = (pred[1,32,2,512]{1,3,2,0:T(8,128)(4,1)S(1)}, pred[1,32,2,512]{1,3,2,0:T(8,128)(4,1)}, u32[]{:S(2)}) copy-start(pred[1,32,2,512]{1,3,2,0:T(8,128)(4,1)} %get-tuple-element.146) | copy-start | bytes 98308
  43.4 3.8 %copy-start.1 = (pred[1,32,2,512]{1,3,2,0:T(8,128)(4,1)S(1)}, pred[1,32,2,512]{1,3,2,0:T(8,128)(4,1)}, u32[]{:S(2)}) copy-start(pred[1,32,2,512]{1,3,2,0:T(8,128)(4,1)} %get-tuple-element.153) | copy-start | bytes 98308
  43.4 3.8 %copy-start.2 = (pred[1,32,2,512]{1,3,2,0:T(8,128)(4,1)S(1)}, pred[1,32,2,512]{1,3,2,0:T(8,128)(4,1)}, u32[]{:S(2)}) copy-start(pred[1,32,2,512]{1,3,2,0:T(8,128)(4,1)} %get-tuple-element.154) | copy-start | bytes 98308
  48.9 5.2 %collective-permute-start.4 = (f32[2,32,1,64]{1,3,0,2:T(8,128)S(1)}, f32[2,32,1,64]{1,3,0,2:T(8,128)S(1)}, u32[]{:S(2)}, u32[]{:S(2)}) collective-permute-start(f32[2,32,1,64]{1,3,0,2:T(8,128)S(1)} %bitcast.273), channel_id=1, source_target_pairs={{0,1},{1,2},{2,3},{3,4},{4,5},{5,6},{6,7},{7,0},{8,9},{9,10},{10,1... | collective-permute-start | bytes 49160 | tf_op jit(solution)/shard_map/ppermute | solution.py:21
  52.7 3.7 %collective-permute-start.5 = (f32[2,32,1,64]{1,3,0,2:T(8,128)S(1)}, f32[2,32,1,64]{1,3,0,2:T(8,128)S(1)}, u32[]{:S(2)}, u32[]{:S(2)}) collective-permute-start(f32[2,32,1,64]{1,3,0,2:T(8,128)S(1)} %bitcast.272), channel_id=1, source_target_pairs={{1,0},{2,1},{3,2},{4,3},{5,4},{6,5},{7,6},{0,7},{9,8},{10,9},{11,1... | collective-permute-start | bytes 49160 | tf_op jit(solution)/shard_map/ppermute | solution.py:22
  56.5 2.9 %copy-start.5 = (f32[1,32,512]{2,1,0:T(8,128)S(1)}, f32[1,32,512]{2,1,0:T(8,128)}, u32[]{:S(2)}) copy-start(f32[1,32,512]{2,1,0:T(8,128)} %get-tuple-element.192) | copy-start | bytes 196612
  57.5 53.9 %collective-permute-start.6 = (f32[2,32,1,512]{1,3,2,0:T(8,128)}, f32[2,32,1,512]{1,3,2,0:T(8,128)S(1)}, u32[]{:S(2)}, u32[]{:S(2)}) collective-permute-start(f32[2,32,1,512]{1,3,2,0:T(8,128)} %get-tuple-element.121), channel_id=1, source_target_pairs={{0,8},{8,16},{16,24},{24,32},{32,40},{40,48},{48,56},{56,64},{64,7... | collective-permute-start | bytes 393224 | tf_op jit(solution)/shard_map/ppermute | solution.py:21
  108.5 15.0 %collective-permute-start.7 = (f32[2,32,1,512]{1,3,2,0:T(8,128)S(1)}, f32[2,32,1,512]{1,3,2,0:T(8,128)S(1)}, u32[]{:S(2)}, u32[]{:S(2)}) collective-permute-start(f32[2,32,1,512]{1,3,2,0:T(8,128)S(1)} %get-tuple-element.120), channel_id=1, source_target_pairs={{8,0},{16,8},{24,16},{32,24},{40,32},{48,40},{56,48},{64,56},{72,6... | collective-permute-start | bytes 393224 | tf_op jit(solution)/shard_map/ppermute | solution.py:22
